TPU v7x, 32 devices: a whole 2x2x4 slice. The times are simulated.
32 devices in a mesh: ka: 8 (over z, y), ga: 4 (over x, core).
Axes of the slice: x: 2, y: 2, z: 4, core: 2. Of those that a mesh axis runs over, the one named last changes fastest.
Arguments:
- x_dens: bfloat16 [32, 64, 1500], P('ka', None, 'ga'), may hold values from -6 to 6
- y_dens: bfloat16 [32, 64, 1500], P('ka', None, 'ga'), may hold values from -0.15625 to 0.15625
- p_dens: bfloat16 [32, 64, 1500], P('ka', None, 'ga'), may hold values from -1 to 1
- coulomb: float32 [1500], P('ga'), may hold values from 0.1 to 2
- screened: bfloat16 [16, 1500, 1500], P('ka', 'ga'), may hold values from -0.15625 to 0.15625
- pairs: int32 [128, 3], P('ka'), may hold values from 0 to 31, as said below
- q_slot: int32 [16], replicated, may hold values from 0 to 15, as said below
Outputs:
- blocks: float32 [128, 4096], P('ka')
- mirrored: float32 [32, 4096], P('ka')
Inputs may be any that keep to these rules, and one draw needn't show every extreme that they name: `pairs`: column 0 of the rows held by index d of ka lies in d * 4 to (d + 1) * 4 - 1; column 1 is any k-point; column 2 is a momentum transfer below 16. Among one index's 16 rows at most 2 have a second k-point held by one same index, and this is reached; at most 2 have q_slot[q] // 2 equal to one same value, and this is reached. `q_slot`: A permutation of the slots; slot s of screened is held by index s // 2 of ka.
All inputs are finite; a program needn't handle non-finite values.
Results may differ from a plain program's by a relative error of at most 0.0014.
Values may be sent and summed in bfloat16 or wider, within the bound.
A program may use at most 192 MiB of HBM per device.

v0:
```python
import jax
import jax.numpy as jnp
from jax import lax
from jax.sharding import PartitionSpec as P

CAPQ = 2
CAPK = 2


def earlier_count(owners):
    places = jnp.arange(owners.shape[0])
    same_owner = owners[:, None] == owners[None, :]
    before = places[:, None] > places[None, :]
    return jnp.sum(jnp.logical_and(same_owner, before).astype(jnp.int32), axis=1)


def per_device(x_dens, y_dens, p_dens, coulomb, screened, pairs, q_slot):
    n_ka = lax.axis_size("ka")
    mine_index = lax.axis_index("ka")
    per_dev, transitions, g_local = x_dens.shape
    q_slots = screened.shape[0]
    pair_rows = pairs.shape[0]
    k_local = pairs[:, 0] - mine_index * per_dev
    partner = pairs[:, 1]
    q_index = pairs[:, 2]
    slot_of = jnp.sum(
        jnp.where(q_index[:, None] == jnp.arange(q_slot.shape[0])[None, :], q_slot[None, :], 0),
        axis=1,
    )
    q_owner = slot_of // q_slots
    q_local = slot_of % q_slots
    q_rank = earlier_count(q_owner)
    q_route = ((q_owner * CAPQ + q_rank)[:, None] == jnp.arange(n_ka * CAPQ)[None, :]).astype(
        jnp.bfloat16
    )
    pick_first = (k_local[:, None] == jnp.arange(per_dev)[None, :]).astype(jnp.bfloat16)
    x_rows = jnp.einsum(
        "jk,kig->jig", pick_first, x_dens, preferred_element_type=jnp.float32
    ).astype(jnp.bfloat16)
    p_rows = jnp.einsum(
        "jk,kig->jig", pick_first, p_dens, preferred_element_type=jnp.float32
    ).astype(jnp.bfloat16)
    send_x = jnp.einsum("js,jig->sig", q_route, x_rows, preferred_element_type=jnp.float32).astype(
        jnp.bfloat16
    )
    send_x = send_x.reshape(n_ka, CAPQ, transitions, g_local)
    send_q = jnp.sum(q_route.astype(jnp.int32) * q_local[:, None], axis=0).reshape(n_ka, CAPQ)
    got_x, got_q = (
        lax.all_to_all(send_x, "ka", split_axis=0, concat_axis=0, tiled=True),
        lax.all_to_all(send_q, "ka", split_axis=0, concat_axis=0, tiled=True),
    )
    chosen = (got_q[:, :, None] == jnp.arange(q_slots)[None, None, :]).astype(jnp.bfloat16)
    stacked = got_x[:, :, None, :, :] * chosen[:, :, :, None, None]
    partial_value = jnp.einsum(
        "ncsig,sgh->hnci", stacked, screened, preferred_element_type=jnp.float32
    )
    half_rows = lax.psum_scatter(
        partial_value.reshape(lax.axis_size("ga") * g_local, n_ka, CAPQ * transitions),
        "ga",
        scatter_dimension=0,
        tiled=True,
    ).astype(jnp.bfloat16)
    returned = lax.all_to_all(half_rows, "ka", split_axis=1, concat_axis=1, tiled=True)
    returned = returned.reshape(g_local, n_ka * CAPQ, transitions)
    u_rows = jnp.einsum(
        "js,gsi->jig", q_route, returned, preferred_element_type=jnp.float32
    ).astype(jnp.bfloat16)
    all_pairs = lax.all_gather(pairs, "ka", axis=0, tiled=True).reshape(n_ka, pair_rows, 3)
    seconds = all_pairs[:, :, 1]
    k_owners = seconds // per_dev
    k_ranks = jax.vmap(earlier_count)(k_owners)
    held_here = k_owners == mine_index
    rank_hot = (k_ranks[:, :, None] == jnp.arange(CAPK)[None, None, :]).astype(jnp.float32)
    local_hot = jnp.logical_and(
        (seconds - mine_index * per_dev)[:, :, None] == jnp.arange(per_dev)[None, None, :],
        held_here[:, :, None],
    ).astype(jnp.float32)
    selector = jnp.einsum("njc,njk->nck", rank_hot, local_hot).astype(jnp.bfloat16)
    send_y = jnp.einsum(
        "nck,kig->ncig", selector, y_dens, preferred_element_type=jnp.float32
    ).astype(jnp.bfloat16)
    send_p = jnp.einsum(
        "nck,kig->ncig", selector, p_dens, preferred_element_type=jnp.float32
    ).astype(jnp.bfloat16)
    got_y, got_p = (
        lax.all_to_all(send_y, "ka", split_axis=0, concat_axis=0, tiled=True),
        lax.all_to_all(send_p, "ka", split_axis=0, concat_axis=0, tiled=True),
    )
    own_rank = earlier_count(partner // per_dev)
    pick_second = (
        (partner // per_dev * CAPK + own_rank)[:, None] == jnp.arange(n_ka * CAPK)[None, :]
    ).astype(jnp.bfloat16)
    y_rows = jnp.einsum(
        "js,sig->jig",
        pick_second,
        got_y.reshape(n_ka * CAPK, transitions, g_local),
        preferred_element_type=jnp.float32,
    ).astype(jnp.bfloat16)
    pp_rows = jnp.einsum(
        "js,sig->jig",
        pick_second,
        got_p.reshape(n_ka * CAPK, transitions, g_local),
        preferred_element_type=jnp.float32,
    ).astype(jnp.bfloat16)
    direct = jnp.einsum("jig,jhg->jih", u_rows, y_rows, preferred_element_type=jnp.float32)
    weighted = p_rows.astype(jnp.float32) * coulomb[None, None, :]
    exchange_term = jnp.einsum(
        "jig,jhg->jih", weighted, pp_rows.astype(jnp.float32), precision=lax.Precision.HIGHEST
    )
    kernel_block = lax.psum(2.0 * exchange_term - direct, "ga")
    blocks = kernel_block.reshape(pair_rows, transitions * transitions)
    flipped = jnp.transpose(kernel_block, (0, 2, 1)).reshape(pair_rows, transitions * transitions)
    selector = (partner[:, None] == jnp.arange(lax.axis_size("ka") * per_dev)[None, :]).astype(
        jnp.float32
    )
    mirrored = lax.psum_scatter(
        jnp.dot(selector.T, flipped, precision=lax.Precision.HIGHEST),
        "ka",
        scatter_dimension=0,
        tiled=True,
    )
    return (blocks, mirrored)


def solution(mesh):
    in_specs = (
        P("ka", None, "ga"),
        P("ka", None, "ga"),
        P("ka", None, "ga"),
        P("ga"),
        P("ka", "ga", None),
        P("ka", None),
        P(),
    )
    out_specs = (P("ka", None), P("ka", None))
    return jax.shard_map(
        per_device, mesh=mesh, in_specs=in_specs, out_specs=out_specs, check_vma=False
    )
```

profile of v0, /device:TPU:0, one launch (start us, length us, event | category | flops | bytes accessed | tf_op | source)
XLA Modules:
  0.0 274.0 jit_solution(15575906817718074861)
XLA Ops:
  9.9 7.3 %all-to-all-start.2 = ((s32[8,1,2]{2,1,0:T(1,128)}), s32[8,1,2]{2,1,0:T(1,128)S(1)}, u32[]{:S(2)}, u32[]{:S(2)}) async-start(s32[8,1,2]{2,1,0:T(1,128)} %bitcast.18), calls=%async_computation.2 | async-start | bytes 8192 | tf_op jit(solution)/shard_map/all_to_all | solution.py:50
  17.2 2.5 convolution_convert_fusion.3
  19.7 2.2 reshape.166
  21.9 1.5 copy.117
  23.6 5.8 %all-to-all-start.1 = ((bf16[8,2,64,375]{3,1,2,0:T(2,128)(2,1)}), bf16[8,2,64,375]{3,1,2,0:T(2,128)(2,1)S(1)}, u32[]{:S(2)}, u32[]{:S(2)}) async-start(bf16[8,2,64,375]{3,1,2,0:T(2,128)(2,1)} %copy.117), calls=%async_computation.1 | async-start | bytes 1572864 | tf_op jit(solution)/shard_map/all_to_all | solution.py:49
  29.5 19.6 %all-to-all-done.1 = bf16[8,2,64,375]{3,1,2,0:T(2,128)(2,1)S(1)} async-done(((bf16[8,2,64,375]{3,1,2,0:T(2,128)(2,1)}), bf16[8,2,64,375]{3,1,2,0:T(2,128)(2,1)S(1)}, u32[]{:S(2)}, u32[]{:S(2)}) %all-to-all-start.1) | async-done | bytes 768032 | tf_op jit(solution)/shard_map/all_to_all | solution.py:49
  49.2 5.0 %fusion = f32[8,2,64,1500,1]{3,2,4,1,0:T(8,128)} fusion(bf16[2,375,1500,1,1]{2,0,1,4,3:T(2,128)(2,1)S(1)} %bitcast.72, bf16[8,2,2]{2,1,0:T(2,128)(2,1)S(1)} %compare_convert_fusion, bf16[8,2,64,375]{3,2,1,0:T(8,128)(2,1)S(1)} %copy.118), kind=kOutput, calls=%fused_computation | convolution fusion | flops 2304768000 | bytes 9162064 | tf_op jit(solution)/shard_map/ncsig,sgh->hnci/dot_general | solution.py:54
  54.2 6.5 %copy.123 = f32[1500,8,128]{2,1,0:T(8,128)} copy(f32[1500,8,128]{0,2,1:T(8,128)} %bitcast.73) | data formatting | bytes 12288000 | tf_op jit(solution)/shard_map/reshape | solution.py:58
  61.4 26.1 %all-gather = s32[8,16,3]{1,2,0:T(4,128)S(1)} all-gather(s32[1,16,3]{1,2,0:T(4,128)S(1)} %bitcast.81), channel_id=1, replica_groups=mesh['ka'=8,'ga'=4] {'ka'}, dimensions={0}, use_global_device_ids=true | all-gather | bytes 1728 | tf_op jit(solution)/shard_map/all_gather | solution.py:68
  89.6 3.5 %all-to-all-start = ((bf16[8,2,64,375]{3,2,1,0:T(8,128)(2,1)}), bf16[8,2,64,375]{3,2,1,0:T(8,128)(2,1)S(1)}, u32[]{:S(2)}, u32[]{:S(2)}) async-start(bf16[8,2,64,375]{3,2,1,0:T(8,128)(2,1)} %copy.111), calls=%async_computation | async-start | bytes 1572864 | tf_op jit(solution)/shard_map/all_to_all | solution.py:87
  94.6 13.4 %all-to-all-done = bf16[8,2,64,375]{3,2,1,0:T(8,128)(2,1)S(1)} async-done(((bf16[8,2,64,375]{3,2,1,0:T(8,128)(2,1)}), bf16[8,2,64,375]{3,2,1,0:T(8,128)(2,1)S(1)}, u32[]{:S(2)}, u32[]{:S(2)}) %all-to-all-start) | async-done | bytes 768032 | tf_op jit(solution)/shard_map/all_to_all | solution.py:87
  108.0 4.2 %all-to-all-start.4 = ((bf16[8,2,64,375]{3,2,1,0:T(8,128)(2,1)}), bf16[8,2,64,375]{3,2,1,0:T(8,128)(2,1)}, u32[]{:S(2)}, u32[]{:S(2)}) async-start(bf16[8,2,64,375]{3,2,1,0:T(8,128)(2,1)} %copy.128), calls=%async_computation.4 | async-start | bytes 1572864 | tf_op jit(solution)/shard_map/all_to_all | solution.py:86
  112.2 5.5 %reduce-scatter.4.cloned.1.call-done = f32[375,8,128]{2,1,0:T(8,128)} async-done(((f32[1500,8,128]{2,1,0:T(8,128)}), f32[375,8,128]{2,1,0:T(8,128)}) %reduce-scatter.4.cloned.1.call-update) | async-done | bytes 1536016
  117.7 1.5 convert_element_type.77
  120.1 9.4 %all-to-all-done.4 = bf16[8,2,64,375]{3,2,1,0:T(8,128)(2,1)} async-done(((bf16[8,2,64,375]{3,2,1,0:T(8,128)(2,1)}), bf16[8,2,64,375]{3,2,1,0:T(8,128)(2,1)}, u32[]{:S(2)}, u32[]{:S(2)}) %all-to-all-start.4) | async-done | bytes 768032 | tf_op jit(solution)/shard_map/all_to_all | solution.py:86
  129.5 4.2 %all-to-all-start.3 = ((bf16[375,8,128]{2,0,1:T(8,128)(2,1)}), bf16[375,8,128]{2,0,1:T(8,128)(2,1)}, u32[]{:S(2)}, u32[]{:S(2)}) async-start(bf16[375,8,128]{2,0,1:T(8,128)(2,1)} %copy.124), calls=%async_computation.3 | async-start | bytes 1540096 | tf_op jit(solution)/shard_map/all_to_all | solution.py:63
  135.0 2.6 convolution_convert_fusion
  137.7 2.3 fusion.6
  140.0 12.0 %all-to-all-done.3 = bf16[375,8,128]{2,0,1:T(8,128)(2,1)} async-done(((bf16[375,8,128]{2,0,1:T(8,128)(2,1)}), bf16[375,8,128]{2,0,1:T(8,128)(2,1)}, u32[]{:S(2)}, u32[]{:S(2)}) %all-to-all-start.3) | async-done | bytes 768032 | tf_op jit(solution)/shard_map/all_to_all | solution.py:63
  152.0 1.5 copy.125
  156.0 32.5 %all-reduce.5.cloned.1.call-done = f32[16,64,64]{2,1,0:T(8,128)} async-done(((f32[16,64,64]{2,1,0:T(8,128)}), f32[16,64,64]{2,1,0:T(8,128)}) %all-reduce.5.cloned.1.call-update) | async-done | bytes 262160 | tf_op jit(solution)/shard_map/psum | solution.py:110
  190.7 2.2 fusion.37
  195.1 70.8 %all-reduce.7.cloned.1.call-done = f32[32,4096]{1,0:T(8,128)} async-done(((f32[32,4096]{1,0:T(8,128)}), f32[32,4096]{1,0:T(8,128)}) %all-reduce.7.cloned.1.call-update) | async-done | bytes 524304
  265.9 1.5 constant_dynamic-slice_fusion
  (58 shorter events, 15.8 us)
Async XLA Ops:
  7.2 42.0 %copy-start = (bf16[2,375,1500]{2,0,1:T(2,128)(2,1)S(1)}, bf16[2,375,1500]{2,0,1:T(2,128)(2,1)}, u32[]{:S(2)}) copy-start(bf16[2,375,1500]{2,0,1:T(2,128)(2,1)} %param.11) | copy-start | bytes 6750004
  9.9 13.7 %all-to-all-start.2 = ((s32[8,1,2]{2,1,0:T(1,128)}), s32[8,1,2]{2,1,0:T(1,128)S(1)}, u32[]{:S(2)}, u32[]{:S(2)}) async-start(s32[8,1,2]{2,1,0:T(1,128)} %bitcast.18), calls=%async_computation.2 | async-start | bytes 8192 | tf_op jit(solution)/shard_map/all_to_all | solution.py:50
  23.6 25.5 %all-to-all-start.1 = ((bf16[8,2,64,375]{3,1,2,0:T(2,128)(2,1)}), bf16[8,2,64,375]{3,1,2,0:T(2,128)(2,1)S(1)}, u32[]{:S(2)}, u32[]{:S(2)}) async-start(bf16[8,2,64,375]{3,1,2,0:T(2,128)(2,1)} %copy.117), calls=%async_computation.1 | async-start | bytes 1572864 | tf_op jit(solution)/shard_map/all_to_all | solution.py:49
  29.4 88.3 %reduce-scatter.4.cloned.1.call-start = ((), (), s32[]{:S(2)}) async-start(), calls=%async_computation.8 | async-start | bytes 7680000
  60.7 0.7 copy-start.6
  60.7 27.4 %copy-start.4 = (bf16[4,64,375]{2,1,0:T(8,128)(2,1)S(1)}, bf16[4,64,375]{2,1,0:T(8,128)(2,1)}, u32[]{:S(2)}) copy-start(bf16[4,64,375]{2,1,0:T(8,128)(2,1)} %param.9) | copy-start | bytes 576004
  88.5 4.6 %copy-start.5 = (bf16[4,64,375]{2,1,0:T(8,128)(2,1)S(1)}, bf16[4,64,375]{2,1,0:T(8,128)(2,1)}, u32[]{:S(2)}) copy-start(bf16[4,64,375]{2,1,0:T(8,128)(2,1)} %param.8) | copy-start | bytes 576004
  89.6 18.4 %all-to-all-start = ((bf16[8,2,64,375]{3,2,1,0:T(8,128)(2,1)}), bf16[8,2,64,375]{3,2,1,0:T(8,128)(2,1)S(1)}, u32[]{:S(2)}, u32[]{:S(2)}) async-start(bf16[8,2,64,375]{3,2,1,0:T(8,128)(2,1)} %copy.111), calls=%async_computation | async-start | bytes 1572864 | tf_op jit(solution)/shard_map/all_to_all | solution.py:87
  108.0 21.6 %all-to-all-start.4 = ((bf16[8,2,64,375]{3,2,1,0:T(8,128)(2,1)}), bf16[8,2,64,375]{3,2,1,0:T(8,128)(2,1)}, u32[]{:S(2)}, u32[]{:S(2)}) async-start(bf16[8,2,64,375]{3,2,1,0:T(8,128)(2,1)} %copy.128), calls=%async_computation.4 | async-start | bytes 1572864 | tf_op jit(solution)/shard_map/all_to_all | solution.py:86
  119.1 14.9 %copy-start.7 = (f32[375]{0:T(512)S(1)}, f32[375]{0:T(512)}, u32[]{:S(2)}) copy-start(f32[375]{0:T(512)} %param.10) | copy-start | bytes 4504
  129.5 22.4 %all-to-all-start.3 = ((bf16[375,8,128]{2,0,1:T(8,128)(2,1)}), bf16[375,8,128]{2,0,1:T(8,128)(2,1)}, u32[]{:S(2)}, u32[]{:S(2)}) async-start(bf16[375,8,128]{2,0,1:T(8,128)(2,1)} %copy.124), calls=%async_computation.3 | async-start | bytes 1540096 | tf_op jit(solution)/shard_map/all_to_all | solution.py:63
  133.7 54.8 %all-reduce.5.cloned.1.call-start = ((), (), s32[]{:S(2)}) async-start(), calls=%async_computation.6 | async-start | bytes 1048576 | tf_op jit(solution)/shard_map/psum | solution.py:110
  153.5 1.1 copy-start.1
  153.5 1.3 copy-start.3
  156.0 109.9 %all-reduce.7.cloned.1.call-start = ((), (), s32[]{:S(2)}) async-start(), calls=%async_computation.7 | async-start | bytes 1048576
  188.5 4.5 %copy-start.8 = (u32[32]{0:T(128)S(1)}, u32[32]{0:T(128)}, u32[]{:S(2)}) copy-start(u32[32]{0:T(128)} %constant.69) | copy-start | bytes 388
  188.5 5.7 %copy-start.2 = (f32[16,64,64]{2,1,0:T(8,128)S(1)}, f32[16,64,64]{2,1,0:T(8,128)}, u32[]{:S(2)}) copy-start(f32[16,64,64]{2,1,0:T(8,128)} %all-reduce.5.cloned.1.call-done) | copy-start | bytes 786436
Sparse Core Ops, SparseCore 0:
  60.9 56.7 reduce-scatter.3
  156.1 32.3 all-reduce.4
  193.1 72.7 all-reduce.6
where the time goes:
time: 275 us; the launch traced here: 274 us
  waiting for transfers between devices  163 us (59%)
  blocking collectives  26.1 us (9%)
  starting transfers between devices  25.2 us (9%)
  local copies, waits for them, and re-layouts  22.1 us (8%)
  matrix products  18.5 us (7%)
  between operations  14.6 us (5%)
  other arithmetic  4.08 us (1%)
    unnamed x5, waiting for transfers between devices  76.3 us
    psum x1, waiting for transfers between devices, per_device(): kernel_block = lax.psum(2.0 * exchange_term - direct, 'ga')  32.5 us
    all_gather x1, blocking collectives, per_device(): lax.all_gather(pairs, 'ka', axis=0, tiled=True).reshape(n_ka, pair_rows, 3)  26.1 us
    all_to_all x1, waiting for transfers between devices, per_device(): lax.all_to_all(send_x, 'ka', split_axis=0, concat_axis=0, tiled=True)  19.6 us
    all_to_all x1, waiting for transfers between devices, per_device(): lax.all_to_all(send_p, 'ka', split_axis=0, concat_axis=0, tiled=True)  13.4 us
    all_to_all x1, waiting for transfers between devices, per_device(): lax.all_to_all(half_rows, 'ka', split_axis=1, concat_axis=1, tiled=True)  12 us
    all_to_all x1, waiting for transfers between devices, per_device(): lax.all_to_all(send_y, 'ka', split_axis=0, concat_axis=0, tiled=True)  9.42 us
    all_to_all x1, starting transfers between devices, per_device(): lax.all_to_all(send_q, 'ka', split_axis=0, concat_axis=0, tiled=True)  7.31 us
  transfers between devices with their start and end apart: 8, of which 8 were waited for; matrix products, arithmetic and copies ran while one was open for 7% of the time, Pallas kernels for 0%

commit v1 on v0

--- a/solution.py
+++ b/solution.py
@@ -107,7 +107,9 @@
     exchange_term = jnp.einsum(
         "jig,jhg->jih", weighted, pp_rows.astype(jnp.float32), precision=lax.Precision.HIGHEST
     )
-    kernel_block = lax.psum(2.0 * exchange_term - direct, "ga")
+    x = 2.0 * exchange_term - direct
+    parts = lax.all_gather(x, "ga", axis=0, tiled=False)
+    kernel_block = parts.sum(axis=0)
     blocks = kernel_block.reshape(pair_rows, transitions * transitions)
     flipped = jnp.transpose(kernel_block, (0, 2, 1)).reshape(pair_rows, transitions * transitions)
     selector = (partner[:, None] == jnp.arange(lax.axis_size("ka") * per_dev)[None, :]).astype(

time: 275 us -> 265 us (0.964)
  waiting for transfers between devices: 163 us -> 152 us
    psum x1 -> x0, waiting for transfers between devices: 32.5 us -> none  [per_device(): kernel_block = lax.psum(2.0 * exchange_term - direct, 'ga')]
    all_gather x0 -> x1, waiting for transfers between devices: none -> 21.7 us  [per_device(): parts = lax.all_gather(x, 'ga', axis=0, tiled=False)]
  transfers between devices with their start and end apart: 8 -> 8, of which waited for: 8 -> 8; matrix products, arithmetic and copies ran while one was open for 7% -> 8% of each run, Pallas kernels for 0% -> 0%
where the time goes in v1:
time: 265 us; the launch traced here: 264 us
  waiting for transfers between devices  152 us (57%)
  blocking collectives  26.1 us (10%)
  starting transfers between devices  25.2 us (10%)
  local copies, waits for them, and re-layouts  21.1 us (8%)
  matrix products  18.6 us (7%)
  between operations  14.6 us (6%)
  other arithmetic  5.97 us (2%)
    unnamed x5, waiting for transfers between devices  76.1 us
    all_gather x1, blocking collectives, per_device(): lax.all_gather(pairs, 'ka', axis=0, tiled=True).reshape(n_ka, pair_rows, 3)  26.1 us
    all_gather x1, waiting for transfers between devices, per_device(): parts = lax.all_gather(x, 'ga', axis=0, tiled=False)  21.7 us
    all_to_all x1, waiting for transfers between devices, per_device(): lax.all_to_all(send_x, 'ka', split_axis=0, concat_axis=0, tiled=True)  19.6 us
    all_to_all x1, waiting for transfers between devices, per_device(): lax.all_to_all(send_p, 'ka', split_axis=0, concat_axis=0, tiled=True)  13.4 us
    all_to_all x1, waiting for transfers between devices, per_device(): lax.all_to_all(half_rows, 'ka', split_axis=1, concat_axis=1, tiled=True)  12 us
    all_to_all x1, waiting for transfers between devices, per_device(): lax.all_to_all(send_y, 'ka', split_axis=0, concat_axis=0, tiled=True)  9.44 us
    all_to_all x1, starting transfers between devices, per_device(): lax.all_to_all(send_q, 'ka', split_axis=0, concat_axis=0, tiled=True)  7.31 us
  transfers between devices with their start and end apart: 8, of which 8 were waited for; matrix products, arithmetic and copies ran while one was open for 8% of the time, Pallas kernels for 0%

profile of v1, /device:TPU:0, one launch (start us, length us, event | category | flops | bytes accessed | tf_op | source)
XLA Modules:
  0.0 263.9 jit_solution(3420602591104036494)
XLA Ops:
  9.9 7.3 %all-to-all-start.2 = ((s32[8,1,2]{2,1,0:T(1,128)}), s32[8,1,2]{2,1,0:T(1,128)S(1)}, u32[]{:S(2)}, u32[]{:S(2)}) async-start(s32[8,1,2]{2,1,0:T(1,128)} %bitcast.18), calls=%async_computation.2 | async-start | bytes 8192 | tf_op jit(solution)/shard_map/all_to_all | solution.py:50
  17.2 2.5 convolution_convert_fusion.3
  19.7 2.2 reshape.166
  21.9 1.5 copy.117
  23.6 5.8 %all-to-all-start.1 = ((bf16[8,2,64,375]{3,1,2,0:T(2,128)(2,1)}), bf16[8,2,64,375]{3,1,2,0:T(2,128)(2,1)S(1)}, u32[]{:S(2)}, u32[]{:S(2)}) async-start(bf16[8,2,64,375]{3,1,2,0:T(2,128)(2,1)} %copy.117), calls=%async_computation.1 | async-start | bytes 1572864 | tf_op jit(solution)/shard_map/all_to_all | solution.py:49
  29.5 19.6 %all-to-all-done.1 = bf16[8,2,64,375]{3,1,2,0:T(2,128)(2,1)S(1)} async-done(((bf16[8,2,64,375]{3,1,2,0:T(2,128)(2,1)}), bf16[8,2,64,375]{3,1,2,0:T(2,128)(2,1)S(1)}, u32[]{:S(2)}, u32[]{:S(2)}) %all-to-all-start.1) | async-done | bytes 768032 | tf_op jit(solution)/shard_map/all_to_all | solution.py:49
  49.2 5.0 %fusion = f32[8,2,64,1500,1]{3,2,4,1,0:T(8,128)} fusion(bf16[2,375,1500,1,1]{2,0,1,4,3:T(2,128)(2,1)S(1)} %bitcast.73, bf16[8,2,2]{2,1,0:T(2,128)(2,1)S(1)} %compare_convert_fusion, bf16[8,2,64,375]{3,2,1,0:T(8,128)(2,1)S(1)} %copy.118), kind=kOutput, calls=%fused_computation | convolution fusion | flops 2304768000 | bytes 9162064 | tf_op jit(solution)/shard_map/ncsig,sgh->hnci/dot_general | solution.py:54
  54.3 6.5 %copy.123 = f32[1500,8,128]{2,1,0:T(8,128)} copy(f32[1500,8,128]{0,2,1:T(8,128)} %bitcast.74) | data formatting | bytes 12288000 | tf_op jit(solution)/shard_map/reshape | solution.py:58
  61.5 26.1 %all-gather.1 = s32[8,16,3]{1,2,0:T(4,128)S(1)} all-gather(s32[1,16,3]{1,2,0:T(4,128)S(1)} %bitcast.83), channel_id=1, replica_groups=mesh['ka'=8,'ga'=4] {'ka'}, dimensions={0}, use_global_device_ids=true | all-gather | bytes 1728 | tf_op jit(solution)/shard_map/all_gather | solution.py:68
  89.6 3.5 %all-to-all-start = ((bf16[8,2,64,375]{3,2,1,0:T(8,128)(2,1)}), bf16[8,2,64,375]{3,2,1,0:T(8,128)(2,1)S(1)}, u32[]{:S(2)}, u32[]{:S(2)}) async-start(bf16[8,2,64,375]{3,2,1,0:T(8,128)(2,1)} %copy.111), calls=%async_computation | async-start | bytes 1572864 | tf_op jit(solution)/shard_map/all_to_all | solution.py:87
  94.6 13.4 %all-to-all-done = bf16[8,2,64,375]{3,2,1,0:T(8,128)(2,1)S(1)} async-done(((bf16[8,2,64,375]{3,2,1,0:T(8,128)(2,1)}), bf16[8,2,64,375]{3,2,1,0:T(8,128)(2,1)S(1)}, u32[]{:S(2)}, u32[]{:S(2)}) %all-to-all-start) | async-done | bytes 768032 | tf_op jit(solution)/shard_map/all_to_all | solution.py:87
  108.0 4.2 %all-to-all-start.4 = ((bf16[8,2,64,375]{3,2,1,0:T(8,128)(2,1)}), bf16[8,2,64,375]{3,2,1,0:T(8,128)(2,1)}, u32[]{:S(2)}, u32[]{:S(2)}) async-start(bf16[8,2,64,375]{3,2,1,0:T(8,128)(2,1)} %copy.128), calls=%async_computation.4 | async-start | bytes 1572864 | tf_op jit(solution)/shard_map/all_to_all | solution.py:86
  112.3 5.4 %reduce-scatter.4.cloned.1.call-done = f32[375,8,128]{2,1,0:T(8,128)} async-done(((f32[1500,8,128]{2,1,0:T(8,128)}), f32[375,8,128]{2,1,0:T(8,128)}) %reduce-scatter.4.cloned.1.call-update) | async-done | bytes 1536016
  120.2 9.4 %all-to-all-done.4 = bf16[8,2,64,375]{3,2,1,0:T(8,128)(2,1)} async-done(((bf16[8,2,64,375]{3,2,1,0:T(8,128)(2,1)}), bf16[8,2,64,375]{3,2,1,0:T(8,128)(2,1)}, u32[]{:S(2)}, u32[]{:S(2)}) %all-to-all-start.4) | async-done | bytes 768032 | tf_op jit(solution)/shard_map/all_to_all | solution.py:86
  129.6 4.2 %all-to-all-start.3 = ((bf16[375,8,128]{2,0,1:T(8,128)(2,1)}), bf16[375,8,128]{2,0,1:T(8,128)(2,1)}, u32[]{:S(2)}, u32[]{:S(2)}) async-start(bf16[375,8,128]{2,0,1:T(8,128)(2,1)} %copy.124), calls=%async_computation.3 | async-start | bytes 1540096 | tf_op jit(solution)/shard_map/all_to_all | solution.py:63
  135.1 2.6 convolution_convert_fusion
  137.7 2.3 fusion.6
  140.1 12.0 %all-to-all-done.3 = bf16[375,8,128]{2,0,1:T(8,128)(2,1)} async-done(((bf16[375,8,128]{2,0,1:T(8,128)(2,1)}), bf16[375,8,128]{2,0,1:T(8,128)(2,1)}, u32[]{:S(2)}, u32[]{:S(2)}) %all-to-all-start.3) | async-done | bytes 768032 | tf_op jit(solution)/shard_map/all_to_all | solution.py:63
  152.0 1.5 copy.125
  156.1 21.7 %all-gather.4.cloned.1.call-done = f32[64,64,64]{2,1,0:T(8,128)} async-done(((f32[16,64,64]{2,1,0:T(8,128)}), f32[64,64,64]{2,1,0:T(8,128)}) %all-gather.4.cloned.1.call-update) | async-done | bytes 1048592 | tf_op jit(solution)/shard_map/all_gather | solution.py:111
  177.8 1.9 reduce_sum.62
  180.8 2.2 fusion.37
  185.2 70.7 %all-reduce.4.cloned.1.call-done = f32[32,4096]{1,0:T(8,128)} async-done(((f32[32,4096]{1,0:T(8,128)}), f32[32,4096]{1,0:T(8,128)}) %all-reduce.4.cloned.1.call-update) | async-done | bytes 524304
  255.8 1.5 constant_dynamic-slice_fusion
  (57 shorter events, 16.2 us)
Async XLA Ops:
  7.2 42.1 %copy-start = (bf16[2,375,1500]{2,0,1:T(2,128)(2,1)S(1)}, bf16[2,375,1500]{2,0,1:T(2,128)(2,1)}, u32[]{:S(2)}) copy-start(bf16[2,375,1500]{2,0,1:T(2,128)(2,1)} %param.11) | copy-start | bytes 6750004
  9.9 13.7 %all-to-all-start.2 = ((s32[8,1,2]{2,1,0:T(1,128)}), s32[8,1,2]{2,1,0:T(1,128)S(1)}, u32[]{:S(2)}, u32[]{:S(2)}) async-start(s32[8,1,2]{2,1,0:T(1,128)} %bitcast.18), calls=%async_computation.2 | async-start | bytes 8192 | tf_op jit(solution)/shard_map/all_to_all | solution.py:50
  23.6 25.5 %all-to-all-start.1 = ((bf16[8,2,64,375]{3,1,2,0:T(2,128)(2,1)}), bf16[8,2,64,375]{3,1,2,0:T(2,128)(2,1)S(1)}, u32[]{:S(2)}, u32[]{:S(2)}) async-start(bf16[8,2,64,375]{3,1,2,0:T(2,128)(2,1)} %copy.117), calls=%async_computation.1 | async-start | bytes 1572864 | tf_op jit(solution)/shard_map/all_to_all | solution.py:49
  29.4 88.3 %reduce-scatter.4.cloned.1.call-start = ((), (), s32[]{:S(2)}) async-start(), calls=%async_computation.8 | async-start | bytes 7680000
  60.8 0.7 copy-start.5
  60.8 27.4 %copy-start.3 = (bf16[4,64,375]{2,1,0:T(8,128)(2,1)S(1)}, bf16[4,64,375]{2,1,0:T(8,128)(2,1)}, u32[]{:S(2)}) copy-start(bf16[4,64,375]{2,1,0:T(8,128)(2,1)} %param.9) | copy-start | bytes 576004
  88.6 4.6 %copy-start.4 = (bf16[4,64,375]{2,1,0:T(8,128)(2,1)S(1)}, bf16[4,64,375]{2,1,0:T(8,128)(2,1)}, u32[]{:S(2)}) copy-start(bf16[4,64,375]{2,1,0:T(8,128)(2,1)} %param.8) | copy-start | bytes 576004
  89.6 18.4 %all-to-all-start = ((bf16[8,2,64,375]{3,2,1,0:T(8,128)(2,1)}), bf16[8,2,64,375]{3,2,1,0:T(8,128)(2,1)S(1)}, u32[]{:S(2)}, u32[]{:S(2)}) async-start(bf16[8,2,64,375]{3,2,1,0:T(8,128)(2,1)} %copy.111), calls=%async_computation | async-start | bytes 1572864 | tf_op jit(solution)/shard_map/all_to_all | solution.py:87
  108.0 21.6 %all-to-all-start.4 = ((bf16[8,2,64,375]{3,2,1,0:T(8,128)(2,1)}), bf16[8,2,64,375]{3,2,1,0:T(8,128)(2,1)}, u32[]{:S(2)}, u32[]{:S(2)}) async-start(bf16[8,2,64,375]{3,2,1,0:T(8,128)(2,1)} %copy.128), calls=%async_computation.4 | async-start | bytes 1572864 | tf_op jit(solution)/shard_map/all_to_all | solution.py:86
  119.2 14.9 %copy-start.6 = (f32[375]{0:T(512)S(1)}, f32[375]{0:T(512)}, u32[]{:S(2)}) copy-start(f32[375]{0:T(512)} %param.10) | copy-start | bytes 4504
  129.6 22.4 %all-to-all-start.3 = ((bf16[375,8,128]{2,0,1:T(8,128)(2,1)}), bf16[375,8,128]{2,0,1:T(8,128)(2,1)}, u32[]{:S(2)}, u32[]{:S(2)}) async-start(bf16[375,8,128]{2,0,1:T(8,128)(2,1)} %copy.124), calls=%async_computation.3 | async-start | bytes 1540096 | tf_op jit(solution)/shard_map/all_to_all | solution.py:63
  133.8 44.0 %all-gather.4.cloned.1.call-start = ((), (), s32[]{:S(2)}) async-start(), calls=%async_computation.6 | async-start | bytes 2621440 | tf_op jit(solution)/shard_map/all_gather | solution.py:111
  153.5 1.1 copy-start.1
  153.5 1.3 copy-start.2
  156.1 99.8 %all-reduce.4.cloned.1.call-start = ((), (), s32[]{:S(2)}) async-start(), calls=%async_computation.7 | async-start | bytes 1048576
  179.7 3.4 %copy-start.7 = (u32[32]{0:T(128)S(1)}, u32[32]{0:T(128)}, u32[]{:S(2)}) copy-start(u32[32]{0:T(128)} %constant.71) | copy-start | bytes 388
Sparse Core Ops, SparseCore 0:
  60.9 56.7 reduce-scatter.3
  156.2 21.5 all-gather.3
  183.1 72.6 all-reduce.3
